TPU v7x, 256 devices: a whole 4x4x8 slice. The times are simulated.
256 devices in a mesh: grp: 32 (over z, y_hi, core), seq: 8 (over y_lo, x).
Axes of the slice: x: 4, y: 4 (y_hi: 2, y_lo: 2; y = y_hi * 2 + y_lo), z: 8, core: 2. Of those that a mesh axis runs over, the one named last changes fastest.
Arguments:
- queries: bfloat16 [65536, 4096], P(('grp', 'seq')), may hold values from -8 to 8
- keys: bfloat16 [65536, 4096], P(('grp', 'seq')), may hold values from -6 to 6
- values: bfloat16 [65536, 4096], P(('grp', 'seq')), may hold values from -6 to 6
- global_pos: int32 [512], P(('grp', 'seq')), may hold values from 0 to 127
- layout: int32 [512, 32], P(('grp', 'seq')), may hold values from 0 to 511, all different within a row
Outputs:
- attended: bfloat16 [65536, 4096], P(('grp', 'seq'))
Inputs may be any that keep to these rules, and one draw needn't show every extreme that they name: `layout`: each row lists 32 different block indices, and every block is listed by some row.
All inputs are finite; a program needn't handle non-finite values.
Results may differ from a plain program's by a relative error of at most 0.0042.
Values may be sent and summed in bfloat16 or wider, within the bound.
A program may use at most 128 MiB of HBM per device.

v0:
```python
import math

import jax
import jax.numpy as jnp
from jax import lax
from jax.experimental import pallas as pl
from jax.experimental.pallas import tpu as pltpu
from jax.sharding import PartitionSpec as P

HEADS = 32
HEAD_DIM = 128
BLOCK = 128
WIDTH = HEADS * HEAD_DIM
GROUPS = 32
SEQS = 8
ROWS = 2 * BLOCK
NBLK = 512
LINKS = 32
CHUNKS = 8
WINDOWS = (0, 0, 2, 3, 5, 7, 8)
PACE = (2, 4, 6, 8, 8)
CHUNK_HEADS = HEADS // CHUNKS
CHUNK_WIDTH = WIDTH // CHUNKS
EXP_SCALE = math.log2(math.e) / math.sqrt(HEAD_DIM)
MESH = pl.DeviceIdType.MESH
NEG = float("-inf")


def kernel(
    gpos_ref, layout_ref, q_hbm, k_hbm, v_hbm, out_ref,
    q_ref, k_ref, v_ref, lk_ref, lv_ref, rk_ref, rv_ref, first_ref, sk_ref, sv_ref,
    acc_ref, peak_ref, total_ref, near_ref, pick_ref, gk_ref, weight_ref, whole_ref, stat_ref, patch_ref,
    load_sem, halo_send, halo_recv, first_send, first_recv, kz_send, kz_recv, vz_send, vz_recv,
    ky_send, ky_recv, vy_send, vy_recv, core_send, core_recv,
):
    grp = lax.axis_index("grp")
    seq = lax.axis_index("seq")
    place = grp * SEQS + seq
    after = lax.rem(place + 1, GROUPS * SEQS)
    before = lax.rem(place + GROUPS * SEQS - 1, GROUPS * SEQS)
    z, y_hi, core = grp // 4, lax.rem(grp // 2, 2), lax.rem(grp, 2)
    y_lo, x = seq // 4, lax.rem(seq, 4)

    def group_at(dz, other_y=False, other_core=False):
        zz = lax.rem(z + dz + 8, 8)
        yy = 1 - y_hi if other_y else y_hi
        cc = 1 - core if other_core else core
        return (zz * 2 + yy) * 2 + cc

    right = (after // SEQS, lax.rem(after, SEQS))
    left = (before // SEQS, lax.rem(before, SEQS))
    x_peers = [(grp, y_lo * 4 + lax.rem(x + d, 4)) for d in (1, 3, 2)]
    y_peer = (grp, (1 - y_lo) * 4 + x)
    y_far = (group_at(0, other_y=True), (1 - y_lo) * 4 + x)
    z_up = (group_at(1), seq)
    z_down = (group_at(-1), seq)
    twin = (group_at(0, other_core=True), seq)

    barrier = pltpu.get_barrier_semaphore()
    partners = [left, right, *x_peers, y_peer, y_far, z_up, z_down, twin]
    for device in partners:
        pl.semaphore_signal(barrier, inc=1, device_id=device, device_id_type=MESH)

    loads = [
        pltpu.make_async_copy(src, dst, load_sem.at[n])
        for n, (src, dst) in enumerate(((k_hbm, k_ref), (v_hbm, v_ref), (q_hbm, q_ref)))
    ]
    for load in loads:
        load.start()
    pl.semaphore_wait(barrier, len(partners))

    def remote(src, dst, send, recv, device):
        return pltpu.make_async_remote_copy(
            src_ref=src, dst_ref=dst, send_sem=send, recv_sem=recv, device_id=device, device_id_type=MESH
        )

    last_rows, first_rows = pl.ds(BLOCK, BLOCK), pl.ds(0, BLOCK)

    def halo(c, side):
        lanes = pl.ds(pl.multiple_of(c * CHUNK_WIDTH, CHUNK_WIDTH), CHUNK_WIDTH)
        rows, device = ((last_rows, right), (first_rows, left))[side]
        return [
            remote(
                src.at[rows, lanes], dst[side].at[:, lanes],
                halo_send.at[2 * n + side, c], halo_recv.at[2 * n + side, c], device,
            )
            for n, (src, dst) in enumerate(((k_hbm, (lk_ref, rk_ref)), (v_hbm, (lv_ref, rv_ref))))
        ]

    turns = (x == 3, x == 0)

    crosses = (turns[0] & (y_lo == 1) & (core == 1), turns[1] & (y_lo == 0) & (core == 0))

    def send_halos(which, first, last):
        for side in range(2):
            @pl.when(which[side])
            def _():
                for c in range(first, last):
                    for copy in halo(c, side)[1 if c == 0 else 0 :]:
                        copy.start()

    for side in range(2):
        halo(0, side)[0].start()

    loads[0].wait()
    loads[1].wait()
    for h in range(HEADS):
        lanes = slice(h * HEAD_DIM, (h + 1) * HEAD_DIM)
        means = [
            jnp.sum(ref[b * BLOCK : (b + 1) * BLOCK, lanes].astype(jnp.float32), axis=0, keepdims=True)
            for ref in (k_ref, v_ref)
            for b in range(2)
        ]
        mean = jnp.concatenate(means, axis=0) * (1.0 / BLOCK)
        spread = jnp.mean(mean * mean, axis=-1, keepdims=True)
        first_ref[seq, :, lanes] = (mean / jnp.sqrt(spread + 1e-06)).astype(jnp.bfloat16)

    started = []

    def go(copy):
        copy.start()
        started.append(copy)
        return copy

    halves = [pl.ds(y_lo * 4 + x, 1), pl.ds((1 - y_lo) * 4 + x, 1)]
    y_copy = go(remote(first_ref.at[halves[0]], first_ref.at[halves[0]], first_send.at[6], first_recv.at[6], y_peer))
    send_halos([~turn for turn in turns], 0, 1)
    x_copies = [
        go(remote(first_ref.at[halves[0]], first_ref.at[halves[0]], first_send.at[n], first_recv.at[n], device))
        for n, device in enumerate(x_peers)
    ]
    y_copy.wait_recv()
    x_copies += [
        go(remote(first_ref.at[halves[1]], first_ref.at[halves[1]], first_send.at[3 + n], first_recv.at[3 + n], device))
        for n, device in enumerate(x_peers)
    ]
    send_halos([~turn for turn in turns], 1, CHUNKS)
    send_halos([turn & ~cross for turn, cross in zip(turns, crosses)], 0, CHUNKS)
    send_halos(crosses, 0, PACE[0])

    lines = lax.broadcasted_iota(jnp.int32, (2 * LINKS, 1), 0)
    index = jnp.zeros((2 * LINKS, 1), jnp.int32)
    for r in range(2 * LINKS):
        index = jnp.where(lines == r, layout_ref[r // LINKS, r % LINKS], index)
    ids = lax.broadcasted_iota(jnp.int32, (2 * LINKS, NBLK), 1)
    pick_ref[...] = jnp.where(ids == index, 1.0, 0.0).astype(jnp.bfloat16)

    loads[2].wait()
    bias_left = jnp.where(place == 0, NEG, 0.0)
    bias_right = jnp.where(place == GROUPS * SEQS - 1, NEG, 0.0)
    to_rows = (((1,), (1,)), ((), ()))
    to_cols = (((1,), (0,)), ((), ()))

    def dot(a, b, dims):
        return lax.dot_general(a, b, dims, preferred_element_type=jnp.float32)

    def chunk_lanes(c):
        return pl.ds(pl.multiple_of(c * CHUNK_WIDTH, CHUNK_WIDTH), CHUNK_WIDTH)

    def head_lanes(c, n):
        return pl.ds(pl.multiple_of(c * CHUNK_WIDTH + n * HEAD_DIM, HEAD_DIM), HEAD_DIM)

    def spread_out(column):
        return jnp.broadcast_to(column, (column.shape[0], HEAD_DIM))

    def window(c, carry):
        for copy in halo(c, 0) + halo(c, 1):
            copy.wait_recv()
        for n in range(CHUNK_HEADS):
            lanes = head_lanes(c, n)
            q = q_ref[:, lanes]
            s_near = dot(q, k_ref[:, lanes], to_rows)
            s_left = dot(q[:BLOCK], lk_ref[:, lanes], to_rows) + bias_left
            s_right = dot(q[BLOCK:], rk_ref[:, lanes], to_rows) + bias_right
            scores = jnp.concatenate([s_near, jnp.concatenate([s_left, s_right], axis=0)], axis=1)
            peak = jnp.max(scores, axis=1, keepdims=True)
            weights = jnp.exp2((scores - peak) * EXP_SCALE)
            rounded = weights.astype(jnp.bfloat16)
            side = rounded[:, ROWS:]
            acc_ref[:, lanes] = dot(rounded[:, :ROWS], v_ref[:, lanes], to_cols) + jnp.concatenate([
                dot(side[:BLOCK], lv_ref[:, lanes], to_cols),
                dot(side[BLOCK:], rv_ref[:, lanes], to_cols),
            ], axis=0)
            peak_ref[:, lanes] = spread_out(peak)
            total_ref[:, lanes] = spread_out(jnp.sum(weights, axis=1, keepdims=True))
        return carry

    def windows(n):
        first, last = WINDOWS[n : n + 2]
        if first < last:
            lax.fori_loop(first, last, window, 0)

    head_of_row = lax.rem(lax.broadcasted_iota(jnp.int32, (2 * HEADS, CHUNK_WIDTH), 0), HEADS)
    head_of_lane = lax.broadcasted_iota(jnp.int32, (2 * HEADS, CHUNK_WIDTH), 1) // HEAD_DIM

    def own_head(c):
        return head_of_row == head_of_lane + c * CHUNK_HEADS

    def use_keys(c, carry):
        lanes = chunk_lanes(c)
        keys = sk_ref[:, lanes]
        gk_ref[:, lanes] = dot(pick_ref[...], keys, to_cols).astype(jnp.bfloat16)
        whole = dot(choose, q_ref[:, lanes], to_cols)
        rows = jnp.concatenate([jnp.broadcast_to(whole[b : b + 1], (HEADS, CHUNK_WIDTH)) for b in range(2)], axis=0)
        rows = jnp.where(own_head(c), rows, 0.0).astype(jnp.bfloat16)
        old = jnp.where(c == 0, 0.0, whole_ref[...])
        whole_ref[...] = old + dot(rows, keys, to_rows)
        return carry

    choose_row = lax.broadcasted_iota(jnp.int32, (8, ROWS), 0)
    choose_col = lax.broadcasted_iota(jnp.int32, (8, ROWS), 1)
    choose = jnp.zeros((8, ROWS), jnp.float32)
    for b in range(2):
        choose = jnp.where((choose_row == b) & (choose_col == b * BLOCK + gpos_ref[b]), 1.0, choose)
    choose = choose.astype(jnp.bfloat16)

    def whole_weights():
        scores = whole_ref[...]
        peak = jnp.max(scores, axis=1, keepdims=True)
        weights = jnp.exp2((scores - peak) * EXP_SCALE)
        stat_ref[0] = spread_out(peak)
        stat_ref[1] = spread_out(jnp.sum(weights, axis=1, keepdims=True))
        whole_ref[...] = weights

    def own_sum(own, value, b):
        rows = slice(b * HEADS, (b + 1) * HEADS)
        return jnp.sum(jnp.where(own[rows], value[rows], 0.0), axis=0, keepdims=True)

    row_ids = lax.broadcasted_iota(jnp.int32, (ROWS, HEAD_DIM), 0)
    whole_row = (row_ids == gpos_ref[0]) | (row_ids == BLOCK + gpos_ref[1])
    link_rows = lax.broadcasted_iota(jnp.int32, (ROWS, 2 * LINKS), 0) // BLOCK
    link_cols = lax.broadcasted_iota(jnp.int32, (ROWS, 2 * LINKS), 1) // LINKS

    def listed(c, carry):
        for n in range(CHUNK_HEADS):
            lanes = head_lanes(c, n)
            scores = dot(q_ref[:, lanes], gk_ref[:, lanes], to_rows)
            scores = jnp.where(link_rows == link_cols, scores, NEG)
            here = peak_ref[:, lanes]
            peak = jnp.maximum(here, spread_out(jnp.max(scores, axis=1, keepdims=True)))
            keep = jnp.exp2((here - peak) * EXP_SCALE)
            weights = jnp.exp2((scores - peak[:, : 2 * LINKS]) * EXP_SCALE)
            total = total_ref[:, lanes] * keep + spread_out(jnp.sum(weights, axis=1, keepdims=True))
            share = 1.0 / total
            weight_ref[c * CHUNK_HEADS + n] = (weights * share[:, : 2 * LINKS]).astype(jnp.bfloat16)
            near_ref[:, lanes] = acc_ref[:, lanes] * (keep * share)
        lanes = chunk_lanes(c)
        own = own_head(c)
        tops, sums = (jnp.tile(stat_ref[n], (1, CHUNK_HEADS)) for n in range(2))
        for b in range(2):
            at = pl.ds(b * BLOCK + gpos_ref[b], 1)
            here, top = peak_ref[at, lanes], own_sum(own, tops, b)
            peak = jnp.maximum(here, top)
            keep = jnp.exp2((here - peak) * EXP_SCALE)
            more = jnp.exp2((top - peak) * EXP_SCALE)
            share = 1.0 / (total_ref[at, lanes] * keep + own_sum(own, sums, b) * more)
            patch_ref[2 * b, :, lanes] = jnp.broadcast_to(acc_ref[at, lanes] * (keep * share), (8, CHUNK_WIDTH))
            patch_ref[2 * b + 1, :, lanes] = jnp.broadcast_to(more * share, (8, CHUNK_WIDTH))
        return carry

    def finish(c, carry):
        lanes = chunk_lanes(c)
        vals = sv_ref[:, lanes]
        chosen = dot(pick_ref[...], vals, to_cols).astype(jnp.bfloat16)
        own = own_head(c)
        acc = dot(whole_ref[...].astype(jnp.bfloat16), vals, to_cols)
        patches = [
            patch_ref[2 * b, 0:1, lanes] + own_sum(own, acc, b) * patch_ref[2 * b + 1, 0:1, lanes] for b in range(2)
        ]
        for n in range(CHUNK_HEADS):
            lanes = head_lanes(c, n)
            part = slice(n * HEAD_DIM, (n + 1) * HEAD_DIM)
            result = near_ref[:, lanes] + dot(weight_ref[c * CHUNK_HEADS + n], chosen[:, part], to_cols)
            patch = jnp.concatenate([jnp.broadcast_to(p[:, part], (BLOCK, HEAD_DIM)) for p in patches], axis=0)
            out_ref[:, lanes] = jnp.where(whole_row, patch, result).astype(jnp.bfloat16)
        return carry

    for copy in x_copies:
        copy.wait_recv()
    def rows_of(group):
        return pl.ds(pl.multiple_of(group * 16, 16), 16)

    mine = rows_of(grp)
    for at, ref in ((0, sk_ref), (2, sv_ref)):
        pieces = [first_ref[d, at : at + 2, :].astype(jnp.float32) for d in range(SEQS)]
        ref[mine, :] = jnp.concatenate(pieces, axis=0).astype(jnp.bfloat16)

    def piece(ref, group, send, recv, device):
        remote(ref.at[rows_of(group)], ref.at[rows_of(group)], send, recv, device).start()

    def arrived(ref, recv):
        pltpu.make_async_copy(ref.at[mine], ref.at[mine], recv).wait()

    def to_twin(ref, group, which, slot):
        piece(ref, group, core_send.at[slot], core_recv.at[which], twin)

    busy = ((x == 0) & (y_hi == 0) & (y_lo == 0)) | ((x == 3) & (y_hi == 1) & (y_lo == 1))
    sign = jnp.where(x == 0, 1, -1)
    ahead, behind = (group_at(sign), seq), (group_at(-sign), seq)

    piece(sk_ref, grp, ky_send, ky_recv, y_far)
    piece(sv_ref, grp, vy_send.at[0], vy_recv.at[0], y_far)
    piece(sv_ref, grp, vz_send.at[0, 0], vz_recv.at[0, 0], ahead)
    piece(sv_ref, grp, vz_send.at[1, 0], vz_recv.at[1, 0], behind)
    piece(sk_ref, grp, kz_send.at[0, 0], kz_recv.at[0, 0], ahead)
    piece(sk_ref, grp, kz_send.at[1, 0], kz_recv.at[1, 0], behind)
    to_twin(sk_ref, grp, 1, 8)
    to_twin(sv_ref, grp, 0, 0)
    arrived(sk_ref, ky_recv)
    far = group_at(0, other_y=True)
    piece(sk_ref, far, kz_send.at[2, 0], kz_recv.at[2, 0], ahead)
    piece(sk_ref, far, kz_send.at[3, 0], kz_recv.at[3, 0], behind)
    to_twin(sk_ref, far, 1, 16)
    send_halos(crosses, PACE[0], PACE[1])
    crossed = [(0, far)]
    for s in range(1, 6):
        for kind, (ref, send, recv, row) in enumerate((
            (sv_ref, vz_send, vz_recv, 0), (sk_ref, kz_send, kz_recv, 0), (sk_ref, kz_send, kz_recv, 2),
        )):
            for side in range(2):
                usual, other = ((3, 4), (4, 3))[side] if kind == 2 else ((4, 5), (3, 2))[side]
                fewest, most = min(usual, other), max(usual, other)
                if s > most:
                    continue
                longer = busy if other > usual else ~busy
                dz = (-sign if side == 0 else sign) * s
                group = group_at(dz, other_y=kind == 2)
                n = {4: 7, 5: 6}.get(s, 2 * s - 1 + side)

                def forward():
                    piece(ref, group, send.at[row + side, s], recv.at[row + side, s], (ahead, behind)[side])

                def pass_on():
                    arrived(ref, recv.at[row + side, s - 1])
                    if s < fewest:
                        forward()
                    elif s < most:
                        pl.when(longer)(forward) if s == fewest else forward()
                    if kind == 0:
                        piece(ref, group, vy_send.at[n], vy_recv.at[n], y_far)
                    to_twin(ref, group, min(kind, 1), kind * 8 + n)

                if s <= fewest:
                    pass_on()
                else:
                    pl.when(longer)(pass_on)
                if kind == 0 and s < 5:
                    if (s, side) != (4, 1):
                        crossed.append((n, group_at(dz, other_y=True)))
        if s + 1 < len(PACE):
            send_halos(crosses, PACE[s], PACE[s + 1])
        windows(s)
        while crossed and (crossed[0][0] < 2 * s - 1 and crossed[0][0] < 6 or s == 5):
            n, group = crossed.pop(0)
            arrived(sv_ref, vy_recv.at[n])
            to_twin(sv_ref, group, 0, 24 + n)
    for which, ref in ((1, sk_ref), (0, sv_ref)):
        half = ref.at[pl.ds(0, NBLK // 2)]
        pltpu.make_async_copy(half, half, core_recv.at[which]).wait()
        if which == 1:
            lax.fori_loop(0, CHUNKS, use_keys, 0)
            whole_weights()
            lax.fori_loop(0, CHUNKS, listed, 0)
    lax.fori_loop(0, CHUNKS, finish, 0)
    for copy in started:
        copy.wait_send()

    def sent(ref, send):
        pltpu.make_async_copy(ref.at[mine], ref.at[mine], send).wait()

    sent(sk_ref, ky_send)
    for n in range(8):
        sent(sv_ref, vy_send.at[n])
    for n in range(32):
        sent(sv_ref, core_send.at[n])
    for ref, send, row, (usual, other) in (
        (sv_ref, vz_send, 0, (4, 5)), (sv_ref, vz_send, 1, (3, 2)), (sk_ref, kz_send, 0, (4, 5)),
        (sk_ref, kz_send, 1, (3, 2)), (sk_ref, kz_send, 2, (3, 4)), (sk_ref, kz_send, 3, (4, 3)),
    ):
        for n in range(max(usual, other)):
            if n < min(usual, other):
                sent(ref, send.at[row, n])
            else:
                pl.when(busy if other > usual else ~busy)(lambda: sent(ref, send.at[row, n]))
    for c in range(CHUNKS):
        for copy in halo(c, 0) + halo(c, 1):
            copy.wait_send()


def shards(queries, keys, values, global_pos, layout):
    bf16 = jnp.bfloat16
    hbm_spec = pl.BlockSpec(memory_space=pltpu.HBM)
    smem_spec = pl.BlockSpec(memory_space=pltpu.SMEM)
    dma = pltpu.SemaphoreType.DMA
    return pl.pallas_call(
        kernel,
        out_shape=jax.ShapeDtypeStruct((ROWS, WIDTH), bf16),
        in_specs=[smem_spec, smem_spec, hbm_spec, hbm_spec, hbm_spec],
        out_specs=pl.BlockSpec(memory_space=pltpu.VMEM),
        scratch_shapes=[
            *[pltpu.VMEM((ROWS, WIDTH), bf16)] * 3,
            *[pltpu.VMEM((BLOCK, WIDTH), bf16)] * 4,
            pltpu.VMEM((SEQS, 4, WIDTH), bf16),
            *[pltpu.VMEM((NBLK, WIDTH), bf16)] * 2,
            *[pltpu.VMEM((ROWS, WIDTH), jnp.float32)] * 4,
            pltpu.VMEM((2 * LINKS, NBLK), bf16),
            pltpu.VMEM((2 * LINKS, WIDTH), bf16),
            pltpu.VMEM((HEADS, ROWS, 2 * LINKS), bf16),
            pltpu.VMEM((2 * HEADS, NBLK), jnp.float32),
            pltpu.VMEM((2, 2 * HEADS, HEAD_DIM), jnp.float32),
            pltpu.VMEM((4, 8, WIDTH), jnp.float32),
            dma((3,)), dma((4, CHUNKS)), dma((4, CHUNKS)), dma((7,)), dma((7,)),
            dma((4, 5)), dma((4, 5)), dma((2, 5)), dma((2, 5)),
            dma, dma, dma((8,)), dma((8,)), dma((32,)), dma((2,)),
        ],
        compiler_params=pltpu.CompilerParams(collective_id=0, has_side_effects=True, vmem_limit_bytes=50 * 1024 * 1024),
    )(global_pos, layout, queries, keys, values)


def solution(mesh):
    rows = P(("grp", "seq"), None)
    in_specs = (rows, rows, rows, P(("grp", "seq")), rows)
    return jax.shard_map(shards, mesh=mesh, in_specs=in_specs, out_specs=rows, check_vma=False)
```

profile of v0, /device:TPU:1, one launch (start us, length us, event | category | flops | bytes accessed | tf_op | source)
XLA Modules:
  0.0 81.1 jit_solution(14713026498176116566)
XLA Ops:
  0.0 0.0 copy-start
  0.0 0.7 copy-done
  0.7 0.0 copy-start.1
  0.7 0.7 copy-done.1
  1.3 78.5 %shard_map.55 = bf16[256,4096]{1,0:T(8,128)(2,1)S(1)} custom-call(s32[2]{0:T(128)S(1)} %copy-done.1, s32[2,32]{1,0:T(2,128)S(1)} %copy-done, bf16[256,4096]{1,0:T(8,128)(2,1)} %q_hbm.1, bf16[256,4096]{1,0:T(8,128)(2,1)} %k_hbm.1, bf16[256,4096]{1,0:T(8,128)(2,1)} %v_hbm.1), custom_call_target="tpu_custom_call" | custom-call | tf_op jit(solution)/shard_map/pallas_call | solution.py:395
  79.8 1.3 %copy.7 = bf16[256,4096]{1,0:T(8,128)(2,1)} copy(bf16[256,4096]{1,0:T(8,128)(2,1)S(1)} %shard_map.55) | data formatting | bytes 4194304
Async XLA Ops:
  0.0 0.7 copy-start
  0.7 0.7 copy-start.1
where the time goes:
time: 81.7 us; the launch traced here: 81.1 us
  Pallas kernels  78.5 us (96%)
  local copies, waits for them, and re-layouts  2.65 us (3%)
    pallas_call x1, Pallas kernels, shards(): pl.pallas_call(kernel, out_shape=jax.ShapeDtypeStruct((ROWS, WIDTH), bf16...  78.5 us
    unnamed x5, local copies, waits for them, and re-layouts  2.65 us

commit v1 on v0

--- a/solution.py
+++ b/solution.py
@@ -18,7 +18,7 @@
 LINKS = 32
 CHUNKS = 8
 WINDOWS = (0, 0, 2, 3, 5, 7, 8)
-PACE = (2, 4, 6, 8, 8)
+PACE = (2, 4, 6, 7, 8)
 CHUNK_HEADS = HEADS // CHUNKS
 CHUNK_WIDTH = WIDTH // CHUNKS
 EXP_SCALE = math.log2(math.e) / math.sqrt(HEAD_DIM)

time: 81.7 us -> 81.7 us (level)
  no operation moved by 1% of the time
where the time goes in v1:
time: 81.7 us; the launch traced here: 81.1 us
  Pallas kernels  78.5 us (96%)
  local copies, waits for them, and re-layouts  2.65 us (3%)
    pallas_call x1, Pallas kernels, shards(): pl.pallas_call(kernel, out_shape=jax.ShapeDtypeStruct((ROWS, WIDTH), bf16...  78.5 us
    unnamed x5, local copies, waits for them, and re-layouts  2.65 us

profile of v1, /device:TPU:1, one launch (start us, length us, event | category | flops | bytes accessed | tf_op | source)
XLA Modules:
  0.0 81.1 jit_solution(17124864185591441958)
XLA Ops:
  0.0 0.0 copy-start
  0.0 0.7 copy-done
  0.7 0.0 copy-start.1
  0.7 0.7 copy-done.1
  1.3 78.5 %shard_map.55 = bf16[256,4096]{1,0:T(8,128)(2,1)S(1)} custom-call(s32[2]{0:T(128)S(1)} %copy-done.1, s32[2,32]{1,0:T(2,128)S(1)} %copy-done, bf16[256,4096]{1,0:T(8,128)(2,1)} %q_hbm.1, bf16[256,4096]{1,0:T(8,128)(2,1)} %k_hbm.1, bf16[256,4096]{1,0:T(8,128)(2,1)} %v_hbm.1), custom_call_target="tpu_custom_call" | custom-call | tf_op jit(solution)/shard_map/pallas_call | solution.py:395
  79.8 1.3 %copy.7 = bf16[256,4096]{1,0:T(8,128)(2,1)} copy(bf16[256,4096]{1,0:T(8,128)(2,1)S(1)} %shard_map.55) | data formatting | bytes 4194304
Async XLA Ops:
  0.0 0.7 copy-start
  0.7 0.7 copy-start.1
